TPU v7x, 16 devices: a whole 2x2x2 slice. The times are simulated.
16 devices in a mesh: ep: 16 (over z, y, x, core).
Axes of the slice: x: 2, y: 2, z: 2, core: 2. Of those that a mesh axis runs over, the one named last changes fastest.
Arguments:
- table_in: float32 [262144, 300], P('ep')
- table_out: float32 [262144, 300], P('ep')
- centers: int32 [65536], P('ep')
- contexts: int32 [65536], P('ep')
- negatives: int32 [65536, 10], P('ep')
Outputs:
- output 1: float32 [], replicated
- output 2: float32 [262144, 300], P('ep')
- output 3: float32 [262144, 300], P('ep')
All inputs are finite; a program needn't handle non-finite values.
Results may differ from a plain program's by a relative error of at most 0.001.
Values sent between devices are 32-bit elements.
A program may use at most 1 GiB of HBM per device.

v0:
```python
import functools

import jax
import jax.numpy as jnp
from jax import lax
from jax.experimental import pallas as pl
from jax.experimental.pallas import tpu as pltpu
from jax.sharding import PartitionSpec as P

LEARN_RATE = 0.5
LANES = 128
ROUNDS = ((768, 768), (1536, 768), (1536, 768), (1152, 384))
EXTRA = (768, 768)
BLOCK_MAX = max(block for _, block in ROUNDS + (EXTRA,))
GROUP = 24
PIECE = 128
VMEM_CAP = 62 * 1024 * 1024


def params():
    return pltpu.CompilerParams(vmem_limit_bytes=VMEM_CAP)


def cost(us):
    return pl.CostEstimate(flops=int(us * 1e8), bytes_accessed=int(us * 1e6), transcendentals=0)


def rows_of(x, n_slab):
    x = x.T
    pad = n_slab * LANES - x.shape[1]
    x = jnp.concatenate([x, jnp.zeros((x.shape[0], pad), jnp.float32)], axis=1)
    return [x[:, k * LANES:(k + 1) * LANES] for k in range(n_slab)]


def spread(src_ref, dst_ref, n_slab):
    cols = src_ref.shape[1]
    for c in range(0, cols, PIECE):
        for k, part in enumerate(rows_of(src_ref[:, c:c + PIECE], n_slab)):
            dst_ref[pl.ds(c * n_slab + k, PIECE, stride=n_slab), :] = part


def gather_back(src_ref, dst_ref, n_slab):
    width, cols = dst_ref.shape
    for c in range(0, cols, PIECE):
        x = [src_ref[pl.ds(c * n_slab + k, PIECE, stride=n_slab), :] for k in range(n_slab)]
        dst_ref[:, c:c + PIECE] = jnp.concatenate(x, axis=1).T[:width]


def to_rows(table_t):
    width, rows = table_t.shape
    n_slab = -(-width // LANES)
    cols = 1024
    return pl.pallas_call(
        lambda x_ref, o_ref: spread(x_ref, o_ref, n_slab),
        grid=(rows // cols,),
        in_specs=[pl.BlockSpec((width, cols), lambda i: (0, i))],
        out_specs=pl.BlockSpec((cols * n_slab, LANES), lambda i: (i, 0)),
        out_shape=jax.ShapeDtypeStruct((rows * n_slab, LANES), jnp.float32),
        compiler_params=params(), cost_estimate=cost(22), name="to_rows",
    )(table_t)


def from_rows(flat, width):
    n_slab = -(-width // LANES)
    rows = flat.shape[0] // n_slab
    cols = 1024
    return pl.pallas_call(
        lambda x_ref, o_ref: gather_back(x_ref, o_ref, n_slab),
        grid=(rows // cols,),
        in_specs=[pl.BlockSpec((cols * n_slab, LANES), lambda i: (i, 0))],
        out_specs=pl.BlockSpec((width, cols), lambda i: (0, i)),
        out_shape=jax.ShapeDtypeStruct((width, rows), jnp.float32),
        compiler_params=params(), cost_estimate=cost(22), name="from_rows",
    )(flat)


def u_gather_kernel(n_slab, row_mask, pay_ref, base_ref, table_ref, *rest):
    *outs, tab, rows, sem = rest
    cp = pltpu.make_async_copy(table_ref, tab, sem)
    cp.start()
    cp.wait()
    base = base_ref[0]
    for out in outs:
        size = out.shape[1]

        def one(g, carry, base=base):
            for k in range(8):
                i = g * 8 + k
                row = pay_ref[base + i]
                rows[pl.ds(i * n_slab, n_slab), :] = tab[pl.ds(row, n_slab), :]
            return carry

        lax.fori_loop(0, size // 8, one, 0)
        gather_back(rows, out, n_slab)
        base = base + size


def u_gather(table_rows, pay, base, sizes, width, n_slab, row_mask):
    return pl.pallas_call(
        functools.partial(u_gather_kernel, n_slab, row_mask),
        grid_spec=pltpu.PrefetchScalarGridSpec(
            num_scalar_prefetch=2, grid=(1,),
            in_specs=[pl.BlockSpec(memory_space=pl.ANY)],
            out_specs=[pl.BlockSpec((width, s), lambda i, pay, base: (0, 0)) for s in sizes],
            scratch_shapes=[pltpu.VMEM(table_rows.shape, jnp.float32),
                            pltpu.VMEM((max(sizes) * n_slab, LANES), jnp.float32),
                            pltpu.SemaphoreType.DMA],
        ),
        out_shape=[jax.ShapeDtypeStruct((width, s), jnp.float32) for s in sizes],
        compiler_params=params(), cost_estimate=cost(40), name="u_gather",
    )(pay, base, table_rows)


def add_rows(pay_ref, base, n_own, g_ref, rows, tab, n_slab, row_mask):
    size = g_ref.shape[1]
    spread(g_ref, rows, n_slab)
    n_here = jnp.clip(n_own - base, 0, size)

    def one(g, carry):
        for k in range(8):
            i = g * 8 + k
            at = pl.ds(pay_ref[base + i], n_slab)
            tab[at, :] = tab[at, :] + rows[pl.ds(i * n_slab, n_slab), :]
        return carry

    lax.fori_loop(0, (n_here + 7) // 8, one, 0)


def u_update_kernel(n_slab, row_mask, n_g, final, pay_ref, base_ref, table_ref, *rest):
    grads, (out, tab, rows, sem) = rest[:n_g], rest[n_g:]
    step = pl.program_id(0)

    @pl.when(step == 0)
    def _():
        cp = pltpu.make_async_copy(table_ref, tab, sem)
        cp.start()
        cp.wait()
        base = base_ref[0]
        for g_ref in grads:
            add_rows(pay_ref, base, base_ref[1], g_ref, rows, tab, n_slab, row_mask)
            base = base + g_ref.shape[1]
        if not final:
            cp = pltpu.make_async_copy(tab, out, sem)
            cp.start()
            cp.wait()

    if final:
        @pl.when(step > 0)
        def _():
            n = out.shape[1] * n_slab
            gather_back(tab.at[pl.ds(pl.multiple_of((step - 1) * n, n), n), :], out, n_slab)


def u_update(table_rows, grads, pay, base, n_slab, row_mask, final_width=None):
    final = final_width is not None
    sizes = [g.shape[1] for g in grads]
    cols = 1024
    rows = table_rows.shape[0] // n_slab
    if final:
        out_spec = pl.BlockSpec((final_width, cols), lambda i, pay, base: (0, jnp.maximum(i - 1, 0)))
        out_shape = jax.ShapeDtypeStruct((final_width, rows), jnp.float32)
    else:
        out_spec = pl.BlockSpec(memory_space=pl.ANY)
        out_shape = jax.ShapeDtypeStruct(table_rows.shape, jnp.float32)
    return pl.pallas_call(
        functools.partial(u_update_kernel, n_slab, row_mask, len(grads), final),
        grid_spec=pltpu.PrefetchScalarGridSpec(
            num_scalar_prefetch=2, grid=(rows // cols + 1 if final else 1,),
            in_specs=[pl.BlockSpec(memory_space=pl.ANY)]
            + [pl.BlockSpec(g.shape, lambda i, pay, base: (0, 0)) for g in grads],
            out_specs=out_spec,
            scratch_shapes=[pltpu.VMEM(table_rows.shape, jnp.float32),
                            pltpu.VMEM((max(sizes) * n_slab, LANES), jnp.float32),
                            pltpu.SemaphoreType.DMA],
        ),
        out_shape=out_shape,
        compiler_params=params(), cost_estimate=cost(45), name="u_update",
    )(pay, base, table_rows, *grads)


def pair_kernel(n_slab, row_bits, pay_ref, start_ref, table_ref, acc_ref, u_ref,
                p_ref, acc_out, loss_ref, tab, acc, urow, prow, u_now, v_now, coef, bits,
                same_slot, same_row1, same_row2, terms, sems):
    step = pl.program_id(0)
    row_mask = (1 << row_bits) - 1
    slot_shift = row_bits + 4

    @pl.when(step == 0)
    def _():
        cp0 = pltpu.make_async_copy(table_ref, tab, sems.at[0])
        cp1 = pltpu.make_async_copy(acc_ref, acc, sems.at[1])
        cp0.start()
        cp1.start()
        loss_ref[...] = jnp.zeros_like(loss_ref)
        cp0.wait()
        cp1.wait()

    spread(u_ref, urow, n_slab)
    prow[...] = jnp.zeros_like(prow)
    first = start_ref[step]
    last = start_ref[step + 1]
    lane_k = lax.broadcasted_iota(jnp.int32, (GROUP, LANES), 0)

    def places(i):
        pay = pay_ref[i]
        return pay, pl.ds(pay & row_mask, n_slab), lax.shift_right_logical(pay, slot_shift)

    def scores(base, half, n_valid):
        top = half * GROUP * n_slab
        for k in range(GROUP):
            pay, row, slot = places(base + k)
            bits[k:k + 1, :] = jnp.full((1, LANES), pay, jnp.int32)
            v_now[top + k * n_slab:top + (k + 1) * n_slab, :] = tab[row, :]
            u_now[top + k * n_slab:top + (k + 1) * n_slab, :] = urow[pl.ds(slot, n_slab), :]
        total = jnp.zeros((GROUP, LANES), jnp.float32)
        for k in range(n_slab):
            at = pl.ds(top + k, GROUP, stride=n_slab)
            total = total + v_now[at, :] * u_now[at, :]
        score = jnp.sum(total, axis=1, keepdims=True)
        word = bits[...]
        sg = jnp.where(((word >> row_bits) & 1) == 1, -1.0, 1.0)
        if n_valid is not None:
            sg = jnp.where(lane_k < n_valid, sg, 0.0)
        x = score * sg
        e = jnp.exp(-jnp.abs(x))
        term = jnp.maximum(x, 0.0) + jnp.log1p(e)
        sig = jnp.where(x >= 0, 1.0, e) / (1.0 + e)
        at = pl.ds(half * GROUP, GROUP)
        terms[at, :] = term if n_valid is None else jnp.where(sg == 0.0, 0.0, term)
        coef[at, :] = (-LEARN_RATE) * sg * sig
        for j, ref in enumerate((same_slot, same_row1, same_row2)):
            ref[at, :] = ((word >> (row_bits + 1 + j)) & 1).astype(jnp.float32)

    def apply(base, half, run, n_valid):
        top = half * GROUP
        loss_ref[...] += terms[top:top + GROUP, :]
        for k in range(0, GROUP, 3):
            deltas, news, rows = [], [], []
            for j in range(k, min(k + 3, GROUP)):
                _, row, slot = places(base + j)
                if n_valid is not None:
                    slot = jnp.where(j < n_valid, slot, BLOCK_MAX * n_slab)
                h = top + j
                gj = coef[h:h + 1, :]
                at = slice(h * n_slab, (h + 1) * n_slab)
                delta = gj * u_now[at, :]
                new = acc[row, :] + delta
                if j > k:
                    new = new + same_row1[h:h + 1, :] * deltas[-1]
                if j > k + 1:
                    new = new + same_row2[h:h + 1, :] * deltas[-2]
                deltas.append(delta)
                news.append(new)
                rows.append(row)
                run = same_slot[h:h + 1, :] * run + gj * v_now[at, :]
                prow[pl.ds(slot, n_slab), :] = run
            for row, new in zip(rows, news):
                acc[row, :] = new
        return run

    def two_groups(gi, run):
        base = first + gi * (2 * GROUP)
        scores(base + GROUP, 1, None)
        run = apply(base, 0, run, None)
        scores(base + 2 * GROUP, 0, None)
        return apply(base + GROUP, 1, run, None)

    def tail_group(gi, run):
        base = tail + gi * GROUP
        n_valid = last - base
        scores(base, 0, n_valid)
        return apply(base, 0, run, n_valid)

    scores(first, 0, None)
    n_two = (last - first) // (2 * GROUP)
    run = lax.fori_loop(0, n_two, two_groups, jnp.zeros((n_slab, LANES), jnp.float32))
    tail = first + n_two * (2 * GROUP)
    lax.fori_loop(0, (last - tail + GROUP - 1) // GROUP, tail_group, run)

    gather_back(prow, p_ref, n_slab)

    @pl.when(step == pl.num_programs(0) - 1)
    def _():
        cp = pltpu.make_async_copy(acc, acc_out, sems.at[0])
        cp.start()
        cp.wait()


def pair_step(table_rows, acc_rows, u_all, pay, starts, block, n_dev, n_slab, row_bits):
    width = u_all.shape[0] // n_dev
    nb = u_all.shape[1] // block
    blk = pl.BlockSpec((width, block), lambda i, pay, starts: (i // nb, i % nb))
    any_spec = pl.BlockSpec(memory_space=pl.ANY)
    return pl.pallas_call(
        functools.partial(pair_kernel, n_slab, row_bits),
        grid_spec=pltpu.PrefetchScalarGridSpec(
            num_scalar_prefetch=2,
            grid=(n_dev * nb,),
            in_specs=[any_spec, any_spec, blk],
            out_specs=[blk, any_spec, pl.BlockSpec((GROUP, LANES), lambda i, pay, starts: (0, 0))],
            scratch_shapes=[pltpu.VMEM(table_rows.shape, jnp.float32),
                            pltpu.VMEM(table_rows.shape, jnp.float32),
                            pltpu.VMEM((BLOCK_MAX * n_slab, LANES), jnp.float32),
                            pltpu.VMEM(((BLOCK_MAX + 8) * n_slab, LANES), jnp.float32),
                            pltpu.VMEM((2 * GROUP * n_slab, LANES), jnp.float32),
                            pltpu.VMEM((2 * GROUP * n_slab, LANES), jnp.float32),
                            pltpu.VMEM((2 * GROUP, LANES), jnp.float32),
                            pltpu.VMEM((GROUP, LANES), jnp.int32),
                            pltpu.VMEM((2 * GROUP, LANES), jnp.float32),
                            pltpu.VMEM((2 * GROUP, LANES), jnp.float32),
                            pltpu.VMEM((2 * GROUP, LANES), jnp.float32),
                            pltpu.VMEM((2 * GROUP, LANES), jnp.float32),
                            pltpu.SemaphoreType.DMA((2,))],
        ),
        out_shape=[jax.ShapeDtypeStruct(u_all.shape, jnp.float32),
                   jax.ShapeDtypeStruct(table_rows.shape, jnp.float32),
                   jax.ShapeDtypeStruct((GROUP, LANES), jnp.float32)],
        compiler_params=params(), cost_estimate=cost(u_all.shape[1] // 8), name="pair_step",
    )(pay, starts, table_rows, acc_rows, u_all)


def solution(mesh):
    group_size = mesh.shape['ep']

    def device_step(table_in, table_out, centers, contexts, negatives):
        rows_dev, width = table_in.shape
        n_pairs, n_neg = negatives.shape
        capacity = (3 * n_pairs * (n_neg + 2)) // (2 * group_size)
        n_slab = -(-width // LANES)
        width8 = -(-width // 8) * 8
        dev_row_bits = (rows_dev - 1).bit_length()
        row_bits = (rows_dev * n_slab - 1).bit_length()
        row_mask = (1 << row_bits) - 1
        pair_bits = (n_pairs - 1).bit_length()
        me = lax.axis_index('ep')
        devs = jnp.arange(group_size, dtype=jnp.int32)

        n_all = n_pairs * group_size
        centers_all = lax.all_gather(centers, 'ep', tiled=True)
        owners_all = centers_all % group_size
        pair_ids = jnp.arange(n_all, dtype=jnp.int32)
        assert n_all * rows_dev <= 2 ** 30
        cen_key = jnp.where(owners_all == me, pair_ids * rows_dev + centers_all // group_size, 2 ** 30)
        cen_rows = (lax.sort(cen_key, is_stable=False) & (rows_dev - 1)) * n_slab
        cen_rows = jnp.concatenate([cen_rows, jnp.zeros((EXTRA[0],), jnp.int32)])
        all_counts = jnp.sum((owners_all.reshape(group_size, 1, n_pairs) == devs[None, :, None]).astype(jnp.int32),
                             axis=2)
        totals = jnp.sum(all_counts, axis=0)
        n_own = jnp.sum(jnp.where(devs == me, totals, 0))
        n_most = jnp.max(totals)

        c_owner = centers % group_size
        one_hot = (c_owner[:, None] == devs[None, :]).astype(jnp.float32)
        tri = jnp.tril(jnp.ones((LANES, LANES), jnp.float32))
        n_sub = n_pairs // LANES
        inner = jnp.einsum('ij,bjc->bic', tri, one_hot.reshape(n_sub, LANES, group_size),
                           precision=lax.Precision.HIGHEST)
        before = jnp.einsum('ij,jc->ic', jnp.tril(jnp.ones((n_sub, n_sub), jnp.float32), -1), inner[:, -1, :],
                            precision=lax.Precision.HIGHEST)
        cum = (inner + before[:, None, :]).reshape(n_pairs, group_size)
        local_rank = (jnp.sum(cum * one_hot, axis=1) - 0.5).astype(jnp.int32)

        place = (c_owner << pair_bits | local_rank) << (dev_row_bits + 1)
        neg_t = negatives.T
        e_ctx = place | (contexts // group_size) << 1 | 1
        e_neg = place[None, :] | (neg_t // group_size) << 1
        entries = jnp.concatenate([e_ctx, e_neg.reshape(n_pairs * n_neg)])
        owners = jnp.concatenate([contexts % group_size, (neg_t % group_size).reshape(n_pairs * n_neg)])
        n_to = jnp.sum((owners[None, :] == devs[:, None]).astype(jnp.int32), axis=1)
        lack = jnp.cumsum(capacity - n_to)
        fill_ids = jnp.arange(capacity * group_size - n_pairs * (n_neg + 1), dtype=jnp.int32)
        fill_owner = jnp.sum((fill_ids[None, :] >= lack[:, None]).astype(jnp.int32), axis=0)
        keys = jnp.concatenate([owners, fill_owner])
        words = jnp.concatenate([entries, jnp.full(fill_ids.shape, -1, jnp.int32)])
        _, words = lax.sort((keys, words), num_keys=1, is_stable=False)
        got = lax.all_to_all(words.reshape(group_size, capacity), 'ep', 0, 0)

        offs = jnp.cumsum(all_counts, axis=0) - all_counts
        owner_of = (got >> (dev_row_bits + 1 + pair_bits)) & (group_size - 1)
        rank = (got >> (dev_row_bits + 1)) & (n_pairs - 1)
        for c in range(group_size):
            rank = rank + jnp.where(owner_of == c, offs[:, c:c + 1], 0)
        n_static = sum(size for size, _ in ROUNDS)
        base = n_static + (rank - n_static) // EXTRA[0] * EXTRA[0]
        size, block = EXTRA
        end = n_static
        for r_size, r_block in reversed(ROUNDS):
            inside = rank < end
            end -= r_size
            base = jnp.where(inside, end, base)
            size = jnp.where(inside, r_size, size)
            block = jnp.where(inside, r_block, block)
        in_round = rank - base
        key = jnp.where(got == -1, 2 ** 30, group_size * base + owner_of * size + in_round)
        in_block = in_round
        for _ in range(max(n // b for n, b in ROUNDS + (EXTRA,)) - 1):
            in_block = jnp.where(in_block >= block, in_block - block, in_block)
        pay = ((got >> 1) & (rows_dev - 1)) * n_slab | (got & 1) << row_bits
        pay = pay | (in_block * n_slab) << (row_bits + 4)
        key, pay = lax.sort((key.reshape(-1), pay.reshape(-1)), num_keys=1, is_stable=False)
        row3 = pay & row_mask
        before = [jnp.concatenate([jnp.full((d,), -1, jnp.int32), row3[:-d]]) for d in (1, 2)]
        key_before = jnp.concatenate([jnp.full((1,), -1, jnp.int32), key[:-1]])
        for j, same in enumerate((key == key_before, row3 == before[0], row3 == before[1])):
            pay = pay | same.astype(jnp.int32) << (row_bits + 1 + j)
        pay = jnp.concatenate([pay, jnp.zeros((LANES,), jnp.int32)])
        assert 3 * GROUP <= LANES and row_bits + 4 + (BLOCK_MAX * n_slab - 1).bit_length() <= 32

        def starts_of(first, n_pair, n_block):
            n = group_size * n_pair // n_block
            bounds = group_size * first + jnp.arange(n + 1, dtype=jnp.int32) * n_block
            return jnp.sum((key[None, :] < bounds[:, None]).astype(jnp.int32), axis=1)

        u_rows = to_rows(table_in.T)
        o_rows = to_rows(table_out.T)
        zero = jnp.int32(0)
        us = u_gather(u_rows, cen_rows, jnp.stack([zero]), [s for s, _ in ROUNDS], width8, n_slab, row_mask)
        acc, grads, loss, first = o_rows, [], jnp.float32(0.0), 0
        for (n_pair, n_block), u in zip(ROUNDS, us):
            u_all = lax.all_gather(u, 'ep', tiled=True)
            p_all, acc, part = pair_step(o_rows, acc, u_all, pay, starts_of(first, n_pair, n_block),
                                         n_block, group_size, n_slab, row_bits)
            grads.append(lax.psum_scatter(p_all, 'ep', scatter_dimension=0, tiled=True))
            loss = loss + jnp.sum(part[:, 0])
            first += n_pair
        new_rows = u_update(u_rows, grads[:-1], cen_rows, jnp.stack([zero, n_own]), n_slab, row_mask)
        last_base = jnp.stack([jnp.int32(first - ROUNDS[-1][0]), n_own])
        new_u = u_update(new_rows, grads[-1:], cen_rows, last_base, n_slab, row_mask, final_width=width)
        new_o = from_rows(acc, width)
        total = lax.psum(loss, 'ep')

        def more(state):
            first, t_u, t_o, t_loss = state
            u, = u_gather(u_rows, cen_rows, jnp.stack([first]), [EXTRA[0]], width8, n_slab, row_mask)
            u_all = lax.all_gather(u, 'ep', tiled=True)
            p_all, t_acc, part = pair_step(o_rows, to_rows(t_o), u_all, pay, starts_of(first, *EXTRA),
                                           EXTRA[1], group_size, n_slab, row_bits)
            grad = lax.psum_scatter(p_all, 'ep', scatter_dimension=0, tiled=True)
            t_u = u_update(to_rows(t_u), [grad], cen_rows, jnp.stack([first, n_own]), n_slab, row_mask,
                           final_width=width)
            return first + EXTRA[0], t_u, from_rows(t_acc, width), t_loss + lax.psum(jnp.sum(part[:, 0]), 'ep')

        _, new_u, new_o, total = lax.while_loop(lambda s: s[0] < n_most, more,
                                                (jnp.int32(first), new_u, new_o, total))
        return total / n_all, new_u.T, new_o.T

    return jax.shard_map(device_step, mesh=mesh,
                         in_specs=(P('ep', None), P('ep', None), P('ep'), P('ep'), P('ep', None)),
                         out_specs=(P(), P('ep', None), P('ep', None)), check_vma=False)
```

profile of v0, /device:TPU:0, one launch (start us, length us, event | category | flops | bytes accessed | tf_op | source)
XLA Modules:
  0.0 1094.9 jit_solution(11997144036513183023)
XLA Ops:
  7.2 15.4 %all_gather.18 = s32[65536]{0:T(1024)S(1)} all-gather(s32[4096]{0:T(1024)} %param.9), channel_id=1, replica_groups=mesh['ep'=16] {'ep'}, dimensions={0}, use_global_device_ids=true | all-gather | bytes 278528 | tf_op jit(solution)/shard_map/all_gather | solution.py:339
  22.9 8.8 sort.37
  31.7 22.8 %to_rows.4.table_ref = f32[49152,128]{1,0:T(8,128)} custom-call(f32[300,16384]{1,0:T(8,128)} %bitcast.65), custom_call_target="tpu_custom_call" | custom-call | flops 2200000000 | bytes 22000000 | tf_op jit(solution)/shard_map/to_rows/pallas_call | solution.py:53
  54.6 25.9 %u_gather.2 = (f32[304,768]{1,0:T(8,128)}, f32[304,1536]{1,0:T(8,128)}, f32[304,1536]{1,0:T(8,128)}, f32[304,1152]{1,0:T(8,128)}) custom-call(s32[66304]{0:T(1024)S(1)} %concatenate.25.pay_ref, s32[1]{0:T(128)} %constant.87.clone.1.base_ref, f32[49152,128]{1,0:T(8,128)} %to_rows.4.table_ref), custom_call_target="tpu_custom_call" | custom-call | flops 4000000000 | bytes 40000000 | tf_op jit(solution)/shard_map/u_gather/pallas_call | solution.py:99
  85.4 47.4 %sort.38 = (s32[73728]{0:T(1024)}, s32[73728]{0:T(1024)}) sort(s32[73728]{0:T(1024)S(1)} %get-tuple-element.162, s32[73728]{0:T(1024)S(1)} %get-tuple-element.163), dimensions={0}, to_apply=%region_7.8 | sort | flops 1253376 | bytes 1179648 | tf_op jit(solution)/shard_map/sort | solution.py:375
  132.8 2.3 all-to-all-start
  147.5 22.7 %to_rows.5.table_ref.acc_ref = f32[49152,128]{1,0:T(8,128)} custom-call(f32[300,16384]{1,0:T(8,128)} %bitcast.66), custom_call_target="tpu_custom_call" | custom-call | flops 2200000000 | bytes 22000000 | tf_op jit(solution)/shard_map/to_rows/pallas_call | solution.py:53
  171.9 2.9 fusion.15
  175.2 44.4 %sort.39 = (s32[73728]{0:T(1024)S(1)}, s32[73728]{0:T(1024)S(1)}) sort(s32[73728]{0:T(1024)S(1)} %fusion.12, s32[73728]{0:T(1024)S(1)} %get-tuple-element.151), dimensions={0}, to_apply=%region_10.11 | sort | flops 1253376 | bytes 1179648 | tf_op jit(solution)/shard_map/sort | solution.py:400
  220.0 1.8 convert_reduce_fusion.4.start_ref
  221.7 93.8 %pair_step.5 = (f32[4864,768]{1,0:T(8,128)}, f32[49152,128]{1,0:T(8,128)}, f32[24,128]{1,0:T(8,128)}) custom-call(s32[73856]{0:T(1024)S(1)} %concatenate.32.pay_ref, s32[17]{0:T(128)} %convert_reduce_fusion.4.start_ref, f32[49152,128]{1,0:T(8,128)} %to_rows.5.table_ref.acc_ref, f32[49152,128]{1,0:T(8,128)} %to_rows.5.table_ref.acc_ref, ...), custom_call_target="tpu_custom_call" | custom-call | flops 9600000000 | bytes 96000000 | tf_op jit(solution)/shard_map/pair_step/pallas_call | solution.py:294
  315.6 4.1 convert_reduce_fusion.2
  319.8 152.4 %pair_step.6 = (f32[4864,1536]{1,0:T(8,128)}, f32[49152,128]{1,0:T(8,128)}, f32[24,128]{1,0:T(8,128)}) custom-call(s32[73856]{0:T(1024)S(1)} %concatenate.32.pay_ref, s32[33]{0:T(128)} %get-tuple-element.108.start_ref, f32[49152,128]{1,0:T(8,128)} %to_rows.5.table_ref.acc_ref, f32[49152,128]{1,0:T(8,128)} %get-tuple-element.90.acc_ref, ...), custom_call_target="tpu_custom_call" | custom-call | flops 19200000000 | bytes 192000000 | tf_op jit(solution)/shard_map/pair_step/pallas_call | solution.py:294
  472.3 144.1 %pair_step.7 = (f32[4864,1536]{1,0:T(8,128)}, f32[49152,128]{1,0:T(8,128)}, f32[24,128]{1,0:T(8,128)}) custom-call(s32[73856]{0:T(1024)S(1)} %concatenate.32.pay_ref, s32[33]{0:T(128)} %get-tuple-element.107.start_ref, f32[49152,128]{1,0:T(8,128)} %to_rows.5.table_ref.acc_ref, f32[49152,128]{1,0:T(8,128)} %get-tuple-element.93.acc_ref, ...), custom_call_target="tpu_custom_call" | custom-call | flops 19200000000 | bytes 192000000 | tf_op jit(solution)/shard_map/pair_step/pallas_call | solution.py:294
  616.5 3.2 convert_reduce_fusion.1.start_ref
  619.7 92.0 %pair_step.8 = (f32[4864,1152]{1,0:T(8,128)}, f32[49152,128]{1,0:T(8,128)}, f32[24,128]{1,0:T(8,128)}) custom-call(s32[73856]{0:T(1024)S(1)} %concatenate.32.pay_ref, s32[49]{0:T(128)} %convert_reduce_fusion.1.start_ref, f32[49152,128]{1,0:T(8,128)} %to_rows.5.table_ref.acc_ref, f32[49152,128]{1,0:T(8,128)} %get-tuple-element.96.acc_ref, ...), custom_call_target="tpu_custom_call" | custom-call | flops 14400000000 | bytes 144000000 | tf_op jit(solution)/shard_map/pair_step/pallas_call | solution.py:294
  712.5 1.3 pad_add_fusion.7.base_ref
  713.8 1.3 pad_add_fusion.6.base_ref
  720.1 54.2 %psum.14 = f32[]{:T(128)} all-reduce(f32[]{:T(128)S(6)} %add.257), channel_id=1, replica_groups=mesh['ep'=16] {'ep'}, use_global_device_ids=true, to_apply=%region_23.24 | all-reduce | flops 1 | bytes 8 | tf_op jit(solution)/shard_map/psum | solution.py:430
  774.3 22.9 %from_rows.2 = f32[300,16384]{1,0:T(8,128)} custom-call(f32[49152,128]{1,0:T(8,128)} %get-tuple-element.99.x_ref), custom_call_target="tpu_custom_call" | custom-call | flops 2200000000 | bytes 22000000 | tf_op jit(solution)/shard_map/from_rows/pallas_call | solution.py:67
  797.2 126.1 %reduce-scatter.10.cloned.1.call-done.rest_2_ = f32[304,1536]{1,0:T(8,128)} async-done(((f32[4864,1536]{1,0:T(8,128)}), f32[304,1536]{1,0:T(8,128)}) %reduce-scatter.10.cloned.1.call-update) | async-done | bytes 1867792 | tf_op jit(solution)/shard_map/reduce_scatter | solution.py:423
  923.3 36.8 %u_update.3.table_ref = f32[49152,128]{1,0:T(8,128)} custom-call(s32[66304]{0:T(1024)S(1)} %concatenate.25.pay_ref, s32[2]{0:T(128)} %pad_add_fusion.7.base_ref, f32[49152,128]{1,0:T(8,128)} %to_rows.4.table_ref, f32[304,768]{1,0:T(8,128)} %reduce-scatter.6.cloned.1.call-done.rest_0_, f32[304,1536]{1,0:T(8,128)} %reduce-scatter.8.cloned.1.call-done.rest_1_, ...), custom_call_target="tpu_custom_call" | custom-call | flops 4499999744 | bytes 45000000 | tf_op jit(solution)/shard_map/u_update/pallas_call | solution.py:165
  960.1 96.3 %reduce-scatter.12.cloned.1.call-done.rest_0_ = f32[304,1152]{1,0:T(8,128)} async-done(((f32[4864,1152]{1,0:T(8,128)}), f32[304,1152]{1,0:T(8,128)}) %reduce-scatter.12.cloned.1.call-update) | async-done | bytes 1400848 | tf_op jit(solution)/shard_map/reduce_scatter | solution.py:423
  1056.5 28.9 %u_update.4 = f32[300,16384]{1,0:T(8,128)} custom-call(s32[66304]{0:T(1024)S(1)} %concatenate.25.pay_ref, s32[2]{0:T(128)} %pad_add_fusion.6.base_ref, f32[49152,128]{1,0:T(8,128)} %u_update.3.table_ref, f32[304,1152]{1,0:T(8,128)} %reduce-scatter.12.cloned.1.call-done.rest_0_), custom_call_target="tpu_custom_call" | custom-call | flops 4499999744 | bytes 45000000 | tf_op jit(solution)/shard_map/u_update/pallas_call | solution.py:165
  (115 shorter events, 23.8 us)
Async XLA Ops:
  7.2 214.6 %all-gather.6.cloned.1.call-start = ((), (), s32[]{:S(2)}) async-start(), calls=%async_computation.6 | async-start | bytes 15876096 | tf_op jit(solution)/shard_map/all_gather | solution.py:420
  54.6 28.0 %copy-start.2 = (s32[4096]{0:T(1024)S(1)}, s32[4096]{0:T(1024)}, u32[]{:S(2)}) copy-start(s32[4096]{0:T(1024)} %param.9) | copy-start | bytes 49156
  54.6 29.0 %copy-start.3 = (s32[4096]{0:T(1024)S(1)}, s32[4096]{0:T(1024)}, u32[]{:S(2)}) copy-start(s32[4096]{0:T(1024)} %param.10) | copy-start | bytes 49156
  54.6 29.1 %copy-start.1 = (s32[4096,10]{0,1:T(8,128)S(1)}, s32[4096,10]{0,1:T(8,128)}, u32[]{:S(2)}) copy-start(s32[4096,10]{0,1:T(8,128)} %param.11) | copy-start | bytes 491524
  80.5 239.3 %all-gather.8.cloned.1.call-start = ((), (), s32[]{:S(2)}) async-start(), calls=%async_computation.8 | async-start | bytes 31752192 | tf_op jit(solution)/shard_map/all_gather | solution.py:420
  81.3 391.0 %all-gather.10.cloned.1.call-start = ((), (), s32[]{:S(2)}) async-start(), calls=%async_computation.10 | async-start | bytes 31752192 | tf_op jit(solution)/shard_map/all_gather | solution.py:420
  82.0 537.7 %all-gather.12.cloned.1.call-start = ((), (), s32[]{:S(2)}) async-start(), calls=%async_computation.12 | async-start | bytes 23814144 | tf_op jit(solution)/shard_map/all_gather | solution.py:420
  132.8 37.3 %all-to-all-start = ((s32[16,1,4608]{2,1,0:T(1,128)}), s32[16,1,4608]{2,1,0:T(1,128)S(1)}, u32[]{:S(2)}, u32[]{:S(2)}) async-start(s32[16,1,4608]{2,1,0:T(1,128)} %bitcast.11), calls=%async_computation.1 | async-start | bytes 589824 | tf_op jit(solution)/shard_map/all_to_all | solution.py:376
  135.1 662.1 %reduce-scatter.6.cloned.1.call-start = ((), (), s32[]{:S(2)}) async-start(), calls=%async_computation.7 | async-start | bytes 15876096 | tf_op jit(solution)/shard_map/reduce_scatter | solution.py:423
  315.6 481.6 %reduce-scatter.8.cloned.1.call-start = ((), (), s32[]{:S(2)}) async-start(), calls=%async_computation.9 | async-start | bytes 31752192 | tf_op jit(solution)/shard_map/reduce_scatter | solution.py:423
  472.2 451.1 %reduce-scatter.10.cloned.1.call-start = ((), (), s32[]{:S(2)}) async-start(), calls=%async_computation.11 | async-start | bytes 31752192 | tf_op jit(solution)/shard_map/reduce_scatter | solution.py:423
  616.4 440.1 %reduce-scatter.12.cloned.1.call-start = ((), (), s32[]{:S(2)}) async-start(), calls=%async_computation.13 | async-start | bytes 23814144 | tf_op jit(solution)/shard_map/reduce_scatter | solution.py:423
  711.7 3.3 copy-start.4
  711.7 3.9 copy-start.5
  711.8 5.8 copy-start.6
  711.8 7.1 copy-start.7
Sparse Core Ops, SparseCore 0:
  80.6 73.0 all-gather.5
  156.6 119.2 all-gather.7
  278.1 119.2 all-gather.9
  399.5 94.3 all-gather.11
  499.2 100.2 reduce-scatter.5
  604.5 157.1 reduce-scatter.7
  766.8 156.4 reduce-scatter.9
  928.2 128.2 reduce-scatter.11
where the time goes:
time: 1100 us; the launch traced here: 1090 us
  Pallas kernels  642 us (58%)
  waiting for transfers between devices  224 us (20%)
  other arithmetic  123 us (11%)
  blocking collectives  69.6 us (6%)
  between operations  19.2 us (2%)
  local copies, waits for them, and re-layouts  11.6 us (1%)
    pallas_call x4, Pallas kernels, pair_step(): pl.pallas_call(functools.partial(pair_kernel, n_slab, row_bits), grid_spe...  482 us
    reduce_scatter x4, waiting for transfers between devices, device_step(): grads.append(lax.psum_scatter(p_all, 'ep', scatter_dimension=0, tiled=True))  222 us
    pallas_call x2, Pallas kernels, u_update(): pl.pallas_call(functools.partial(u_update_kernel, n_slab, row_mask, len(g...  65.8 us
    psum x1, blocking collectives, device_step(): total = lax.psum(loss, 'ep')  54.2 us
    sort x1, other arithmetic, device_step(): _, words = lax.sort((keys, words), num_keys=1, is_stable=False)  47.4 us
    pallas_call x2, Pallas kernels, to_rows(): pl.pallas_call(lambda x_ref, o_ref: spread(x_ref, o_ref, n_slab), grid=(r...  45.5 us
    sort x1, other arithmetic, device_step(): lax.sort((key.reshape(-1), pay.reshape(-1)), num_keys=1, is_stable=False)  44.4 us
    pallas_call x1, Pallas kernels, u_gather(): pl.pallas_call(functools.partial(u_gather_kernel, n_slab, row_mask), grid...  25.9 us
  transfers between devices with their start and end apart: 9, of which 2 were waited for; matrix products, arithmetic and copies ran while one was open for 12% of the time, Pallas kernels for 52%

commit v1 on v0

--- a/solution.py
+++ b/solution.py
@@ -9,7 +9,7 @@
 
 LEARN_RATE = 0.5
 LANES = 128
-ROUNDS = ((768, 768), (1536, 768), (1536, 768), (1152, 384))
+ROUNDS = ((1920, 640), (3072, 768))
 EXTRA = (768, 768)
 BLOCK_MAX = max(block for _, block in ROUNDS + (EXTRA,))
 GROUP = 24
@@ -74,44 +74,48 @@
     )(flat)
 
 
-def u_gather_kernel(n_slab, row_mask, pay_ref, base_ref, table_ref, *rest):
-    *outs, tab, rows, sem = rest
-    cp = pltpu.make_async_copy(table_ref, tab, sem)
-    cp.start()
-    cp.wait()
-    base = base_ref[0]
-    for out in outs:
-        size = out.shape[1]
-
-        def one(g, carry, base=base):
-            for k in range(8):
-                i = g * 8 + k
-                row = pay_ref[base + i]
-                rows[pl.ds(i * n_slab, n_slab), :] = tab[pl.ds(row, n_slab), :]
-            return carry
-
-        lax.fori_loop(0, size // 8, one, 0)
-        gather_back(rows, out, n_slab)
-        base = base + size
-
-
-def u_gather(table_rows, pay, base, sizes, width, n_slab, row_mask):
-    return pl.pallas_call(
-        functools.partial(u_gather_kernel, n_slab, row_mask),
+def u_gather_kernel(n_slab, pay_ref, base_ref, table_ref, *rest):
+    *outs, tab, rows = rest
+    step = pl.program_id(0)
+    part = table_ref.shape[1] * n_slab
+    spread(table_ref, tab.at[pl.ds(pl.multiple_of(step * part, part), part), :], n_slab)
+
+    @pl.when(step == pl.num_programs(0) - 1)
+    def _():
+        base = base_ref[0]
+        for out in outs:
+            size = out.shape[1]
+
+            def one(g, carry, base=base):
+                for k in range(8):
+                    i = g * 8 + k
+                    row = pay_ref[base + i]
+                    rows[pl.ds(i * n_slab, n_slab), :] = tab[pl.ds(row, n_slab), :]
+                return carry
+
+            lax.fori_loop(0, size // 8, one, 0)
+            gather_back(rows, out, n_slab)
+            base = base + size
+
+
+def u_gather(table_t, pay, base, sizes, width8, n_slab):
+    width, n_rows = table_t.shape
+    cols = 1024
+    return pl.pallas_call(
+        functools.partial(u_gather_kernel, n_slab),
         grid_spec=pltpu.PrefetchScalarGridSpec(
-            num_scalar_prefetch=2, grid=(1,),
-            in_specs=[pl.BlockSpec(memory_space=pl.ANY)],
-            out_specs=[pl.BlockSpec((width, s), lambda i, pay, base: (0, 0)) for s in sizes],
-            scratch_shapes=[pltpu.VMEM(table_rows.shape, jnp.float32),
-                            pltpu.VMEM((max(sizes) * n_slab, LANES), jnp.float32),
-                            pltpu.SemaphoreType.DMA],
+            num_scalar_prefetch=2, grid=(n_rows // cols,),
+            in_specs=[pl.BlockSpec((width, cols), lambda i, pay, base: (0, i))],
+            out_specs=[pl.BlockSpec((width8, s), lambda i, pay, base: (0, 0)) for s in sizes],
+            scratch_shapes=[pltpu.VMEM((n_rows * n_slab, LANES), jnp.float32),
+                            pltpu.VMEM((max(sizes) * n_slab, LANES), jnp.float32)],
         ),
-        out_shape=[jax.ShapeDtypeStruct((width, s), jnp.float32) for s in sizes],
+        out_shape=[jax.ShapeDtypeStruct((width8, s), jnp.float32) for s in sizes],
         compiler_params=params(), cost_estimate=cost(40), name="u_gather",
-    )(pay, base, table_rows)
-
-
-def add_rows(pay_ref, base, n_own, g_ref, rows, tab, n_slab, row_mask):
+    )(pay, base, table_t)
+
+
+def add_rows(pay_ref, base, n_own, g_ref, rows, tab, n_slab):
     size = g_ref.shape[1]
     spread(g_ref, rows, n_slab)
     n_here = jnp.clip(n_own - base, 0, size)
@@ -126,8 +130,44 @@
     lax.fori_loop(0, (n_here + 7) // 8, one, 0)
 
 
-def u_update_kernel(n_slab, row_mask, n_g, final, pay_ref, base_ref, table_ref, *rest):
+def u_update_kernel(n_slab, n_g, pay_ref, base_ref, table_ref, *rest):
     grads, (out, tab, rows, sem) = rest[:n_g], rest[n_g:]
+    step = pl.program_id(0)
+    part = table_ref.shape[1] * n_slab
+    spread(table_ref, tab.at[pl.ds(pl.multiple_of(step * part, part), part), :], n_slab)
+
+    @pl.when(step == pl.num_programs(0) - 1)
+    def _():
+        base = base_ref[0]
+        for g_ref in grads:
+            add_rows(pay_ref, base, base_ref[1], g_ref, rows, tab, n_slab)
+            base = base + g_ref.shape[1]
+        cp = pltpu.make_async_copy(tab, out, sem)
+        cp.start()
+        cp.wait()
+
+
+def u_update(table_t, grads, pay, base, n_slab):
+    width, n_rows = table_t.shape
+    cols = 1024
+    sizes = [g.shape[1] for g in grads]
+    return pl.pallas_call(
+        functools.partial(u_update_kernel, n_slab, len(grads)),
+        grid_spec=pltpu.PrefetchScalarGridSpec(
+            num_scalar_prefetch=2, grid=(n_rows // cols,),
+            in_specs=[pl.BlockSpec((width, cols), lambda i, pay, base: (0, i))]
+            + [pl.BlockSpec(g.shape, lambda i, pay, base: (0, 0)) for g in grads],
+            out_specs=pl.BlockSpec(memory_space=pl.ANY),
+            scratch_shapes=[pltpu.VMEM((n_rows * n_slab, LANES), jnp.float32),
+                            pltpu.VMEM((max(sizes) * n_slab, LANES), jnp.float32),
+                            pltpu.SemaphoreType.DMA],
+        ),
+        out_shape=jax.ShapeDtypeStruct((n_rows * n_slab, LANES), jnp.float32),
+        compiler_params=params(), cost_estimate=cost(45), name="u_update",
+    )(pay, base, table_t, *grads)
+
+
+def u_finish_kernel(n_slab, pay_ref, base_ref, table_ref, g_ref, out, tab, rows, sem):
     step = pl.program_id(0)
 
     @pl.when(step == 0)
@@ -135,47 +175,31 @@
         cp = pltpu.make_async_copy(table_ref, tab, sem)
         cp.start()
         cp.wait()
-        base = base_ref[0]
-        for g_ref in grads:
-            add_rows(pay_ref, base, base_ref[1], g_ref, rows, tab, n_slab, row_mask)
-            base = base + g_ref.shape[1]
-        if not final:
-            cp = pltpu.make_async_copy(tab, out, sem)
-            cp.start()
-            cp.wait()
-
-    if final:
-        @pl.when(step > 0)
-        def _():
-            n = out.shape[1] * n_slab
-            gather_back(tab.at[pl.ds(pl.multiple_of((step - 1) * n, n), n), :], out, n_slab)
-
-
-def u_update(table_rows, grads, pay, base, n_slab, row_mask, final_width=None):
-    final = final_width is not None
-    sizes = [g.shape[1] for g in grads]
+        add_rows(pay_ref, base_ref[0], base_ref[1], g_ref, rows, tab, n_slab)
+
+    @pl.when(step > 0)
+    def _():
+        n = out.shape[1] * n_slab
+        gather_back(tab.at[pl.ds(pl.multiple_of((step - 1) * n, n), n), :], out, n_slab)
+
+
+def u_finish(table_rows, grad, pay, base, n_slab, width):
     cols = 1024
-    rows = table_rows.shape[0] // n_slab
-    if final:
-        out_spec = pl.BlockSpec((final_width, cols), lambda i, pay, base: (0, jnp.maximum(i - 1, 0)))
-        out_shape = jax.ShapeDtypeStruct((final_width, rows), jnp.float32)
-    else:
-        out_spec = pl.BlockSpec(memory_space=pl.ANY)
-        out_shape = jax.ShapeDtypeStruct(table_rows.shape, jnp.float32)
-    return pl.pallas_call(
-        functools.partial(u_update_kernel, n_slab, row_mask, len(grads), final),
+    n_rows = table_rows.shape[0] // n_slab
+    return pl.pallas_call(
+        functools.partial(u_finish_kernel, n_slab),
         grid_spec=pltpu.PrefetchScalarGridSpec(
-            num_scalar_prefetch=2, grid=(rows // cols + 1 if final else 1,),
-            in_specs=[pl.BlockSpec(memory_space=pl.ANY)]
-            + [pl.BlockSpec(g.shape, lambda i, pay, base: (0, 0)) for g in grads],
-            out_specs=out_spec,
+            num_scalar_prefetch=2, grid=(n_rows // cols + 1,),
+            in_specs=[pl.BlockSpec(memory_space=pl.ANY),
+                      pl.BlockSpec(grad.shape, lambda i, pay, base: (0, 0))],
+            out_specs=pl.BlockSpec((width, cols), lambda i, pay, base: (0, jnp.maximum(i - 1, 0))),
             scratch_shapes=[pltpu.VMEM(table_rows.shape, jnp.float32),
-                            pltpu.VMEM((max(sizes) * n_slab, LANES), jnp.float32),
+                            pltpu.VMEM((grad.shape[1] * n_slab, LANES), jnp.float32),
                             pltpu.SemaphoreType.DMA],
         ),
-        out_shape=out_shape,
-        compiler_params=params(), cost_estimate=cost(45), name="u_update",
-    )(pay, base, table_rows, *grads)
+        out_shape=jax.ShapeDtypeStruct((width, n_rows), jnp.float32),
+        compiler_params=params(), cost_estimate=cost(30), name="u_finish",
+    )(pay, base, table_rows, grad)
 
 
 def pair_kernel(n_slab, row_bits, pay_ref, start_ref, table_ref, acc_ref, u_ref,
@@ -411,10 +435,9 @@
             bounds = group_size * first + jnp.arange(n + 1, dtype=jnp.int32) * n_block
             return jnp.sum((key[None, :] < bounds[:, None]).astype(jnp.int32), axis=1)
 
-        u_rows = to_rows(table_in.T)
         o_rows = to_rows(table_out.T)
         zero = jnp.int32(0)
-        us = u_gather(u_rows, cen_rows, jnp.stack([zero]), [s for s, _ in ROUNDS], width8, n_slab, row_mask)
+        us = u_gather(table_in.T, cen_rows, jnp.stack([zero]), [s for s, _ in ROUNDS], width8, n_slab)
         acc, grads, loss, first = o_rows, [], jnp.float32(0.0), 0
         for (n_pair, n_block), u in zip(ROUNDS, us):
             u_all = lax.all_gather(u, 'ep', tiled=True)
@@ -423,21 +446,20 @@
             grads.append(lax.psum_scatter(p_all, 'ep', scatter_dimension=0, tiled=True))
             loss = loss + jnp.sum(part[:, 0])
             first += n_pair
-        new_rows = u_update(u_rows, grads[:-1], cen_rows, jnp.stack([zero, n_own]), n_slab, row_mask)
+        new_rows = u_update(table_in.T, grads[:-1], cen_rows, jnp.stack([zero, n_own]), n_slab)
         last_base = jnp.stack([jnp.int32(first - ROUNDS[-1][0]), n_own])
-        new_u = u_update(new_rows, grads[-1:], cen_rows, last_base, n_slab, row_mask, final_width=width)
+        new_u = u_finish(new_rows, grads[-1], cen_rows, last_base, n_slab, width)
         new_o = from_rows(acc, width)
         total = lax.psum(loss, 'ep')
 
         def more(state):
             first, t_u, t_o, t_loss = state
-            u, = u_gather(u_rows, cen_rows, jnp.stack([first]), [EXTRA[0]], width8, n_slab, row_mask)
+            u, = u_gather(table_in.T, cen_rows, jnp.stack([first]), [EXTRA[0]], width8, n_slab)
             u_all = lax.all_gather(u, 'ep', tiled=True)
             p_all, t_acc, part = pair_step(o_rows, to_rows(t_o), u_all, pay, starts_of(first, *EXTRA),
                                            EXTRA[1], group_size, n_slab, row_bits)
             grad = lax.psum_scatter(p_all, 'ep', scatter_dimension=0, tiled=True)
-            t_u = u_update(to_rows(t_u), [grad], cen_rows, jnp.stack([first, n_own]), n_slab, row_mask,
-                           final_width=width)
+            t_u = from_rows(u_update(t_u, [grad], cen_rows, jnp.stack([first, n_own]), n_slab), width)
             return first + EXTRA[0], t_u, from_rows(t_acc, width), t_loss + lax.psum(jnp.sum(part[:, 0]), 'ep')
 
         _, new_u, new_o, total = lax.while_loop(lambda s: s[0] < n_most, more,

time: 1100 us -> 1010 us (0.918)
  Pallas kernels: 642 us -> 565 us
  waiting for transfers between devices: 224 us -> 202 us
  starting transfers between devices: 3.05 us -> 14.6 us
    pallas_call x4 -> x2, Pallas kernels: 482 us -> 412 us  [pair_step(): pl.pallas_call(functools.partial(pair_kernel, n_slab, row_bits), grid_spe...]
    reduce_scatter x4 -> x2, waiting for transfers between devices: 222 us -> 186 us  [device_step(): grads.append(lax.psum_scatter(p_all, 'ep', scatter_dimension=0, tiled=True))]
    pallas_call x2 -> x1, Pallas kernels: 45.5 us -> 22.7 us  [to_rows(): pl.pallas_call(lambda x_ref, o_ref: spread(x_ref, o_ref, n_slab), grid=(r...]
    pallas_call x3, Pallas kernels: 91.7 us -> 107 us  [the longest x1 36.8 us: u_finish(): pl.pallas_call(functools.partial(u_finish_kernel, n_slab), grid_spec=pltp...]
    all_gather x4 -> x2, waiting for transfers between devices: 0.02 us -> 15.1 us  [device_step(): u_all = lax.all_gather(u, 'ep', tiled=True)]
    reduce_scatter x4 -> x2, starting transfers between devices: 0.58 us -> 12.2 us  [device_step(): grads.append(lax.psum_scatter(p_all, 'ep', scatter_dimension=0, tiled=True))]
  transfers between devices with their start and end apart: 9 -> 5, of which waited for: 2 -> 2; matrix products, arithmetic and copies ran while one was open for 12% -> 12% of each run, Pallas kernels for 52% -> 49%
where the time goes in v1:
time: 1010 us; the launch traced here: 1000 us
  Pallas kernels  565 us (56%)
  waiting for transfers between devices  202 us (20%)
  other arithmetic  120 us (12%)
  blocking collectives  71.7 us (7%)
  between operations  17.7 us (2%)
  starting transfers between devices  14.6 us (1%)
  local copies, waits for them, and re-layouts  11.6 us (1%)
    pallas_call x2, Pallas kernels, pair_step(): pl.pallas_call(functools.partial(pair_kernel, n_slab, row_bits), grid_spe...  412 us
    reduce_scatter x2, waiting for transfers between devices, device_step(): grads.append(lax.psum_scatter(p_all, 'ep', scatter_dimension=0, tiled=True))  186 us
    psum x1, blocking collectives, device_step(): total = lax.psum(loss, 'ep')  56.2 us
    sort x1, other arithmetic, device_step(): _, words = lax.sort((keys, words), num_keys=1, is_stable=False)  47.5 us
    sort x1, other arithmetic, device_step(): lax.sort((key.reshape(-1), pay.reshape(-1)), num_keys=1, is_stable=False)  44.4 us
    pallas_call x1, Pallas kernels, u_finish(): pl.pallas_call(functools.partial(u_finish_kernel, n_slab), grid_spec=pltp...  36.8 us
    pallas_call x1, Pallas kernels, u_update(): pl.pallas_call(functools.partial(u_update_kernel, n_slab, len(grads)), gr...  36.6 us
    pallas_call x1, Pallas kernels, u_gather(): pl.pallas_call(functools.partial(u_gather_kernel, n_slab), grid_spec=pltp...  33.6 us
  transfers between devices with their start and end apart: 5, of which 2 were waited for; matrix products, arithmetic and copies ran while one was open for 12% of the time, Pallas kernels for 49%

profile of v1, /device:TPU:0, one launch (start us, length us, event | category | flops | bytes accessed | tf_op | source)
XLA Modules:
  0.0 1003.1 jit_solution(5032480129986380803)
XLA Ops:
  7.2 15.5 %all_gather.12 = s32[65536]{0:T(1024)S(1)} all-gather(s32[4096]{0:T(1024)} %param.9), channel_id=1, replica_groups=mesh['ep'=16] {'ep'}, dimensions={0}, use_global_device_ids=true | all-gather | bytes 278528 | tf_op jit(solution)/shard_map/all_gather | solution.py:363
  23.0 8.8 sort.37
  31.9 33.6 %u_gather.2 = (f32[304,1920]{1,0:T(8,128)}, f32[304,3072]{1,0:T(8,128)}) custom-call(s32[66304]{0:T(1024)S(1)} %concatenate.25.pay_ref, s32[1]{0:T(128)} %constant.93.clone.1.base_ref, f32[300,16384]{1,0:T(8,128)} %bitcast.65), custom_call_target="tpu_custom_call" | custom-call | flops 4000000000 | bytes 40000000 | tf_op jit(solution)/shard_map/u_gather/pallas_call | solution.py:104
  69.0 47.5 %sort.38 = (s32[73728]{0:T(1024)}, s32[73728]{0:T(1024)}) sort(s32[73728]{0:T(1024)S(1)} %get-tuple-element.144, s32[73728]{0:T(1024)S(1)} %get-tuple-element.145), dimensions={0}, to_apply=%region_7.8 | sort | flops 1253376 | bytes 1179648 | tf_op jit(solution)/shard_map/sort | solution.py:399
  116.5 2.3 all-to-all-start
  118.8 12.1 %reduce-scatter.4.cloned.1.call-start = ((), (), s32[]{:S(2)}) async-start(), calls=%async_computation.5 | async-start | bytes 39690240 | tf_op jit(solution)/shard_map/reduce_scatter | solution.py:446
  131.0 0.9 convert_reduce_fusion.3
  136.3 0.8 broadcast_in_dim.259
  142.8 22.7 %to_rows.2.table_ref.acc_ref = f32[49152,128]{1,0:T(8,128)} custom-call(f32[300,16384]{1,0:T(8,128)} %bitcast.71), custom_call_target="tpu_custom_call" | custom-call | flops 2200000000 | bytes 22000000 | tf_op jit(solution)/shard_map/to_rows/pallas_call | solution.py:53
  165.5 0.9 compare_reduce_fusion
  167.3 2.8 fusion.8
  170.5 44.4 %sort.39 = (s32[73728]{0:T(1024)S(1)}, s32[73728]{0:T(1024)S(1)}) sort(s32[73728]{0:T(1024)S(1)} %add_select_fusion.5, s32[73728]{0:T(1024)S(1)} %get-tuple-element.133), dimensions={0}, to_apply=%region_10.11 | sort | flops 1253376 | bytes 1179648 | tf_op jit(solution)/shard_map/sort | solution.py:424
  215.3 3.2 convert_reduce_fusion.2.start_ref
  218.5 194.7 %pair_step.3 = (f32[4864,1920]{1,0:T(8,128)}, f32[49152,128]{1,0:T(8,128)}, f32[24,128]{1,0:T(8,128)}) custom-call(s32[73856]{0:T(1024)S(1)} %concatenate.32.pay_ref, s32[49]{0:T(128)} %convert_reduce_fusion.2.start_ref, f32[49152,128]{1,0:T(8,128)} %to_rows.2.table_ref.acc_ref, f32[49152,128]{1,0:T(8,128)} %to_rows.2.table_ref.acc_ref, ...), custom_call_target="tpu_custom_call" | custom-call | flops 24000000000 | bytes 240000000 | tf_op jit(solution)/shard_map/pair_step/pallas_call | solution.py:318
  413.3 4.0 convert_reduce_fusion.1.start_ref
  417.3 15.1 %all-gather.6.cloned.1.call-done.u_ref = f32[4864,3072]{1,0:T(8,128)} async-done(((f32[304,3072]{1,0:T(8,128)}), f32[4864,3072]{1,0:T(8,128)}) %all-gather.6.cloned.1.call-update) | async-done | bytes 59768848 | tf_op jit(solution)/shard_map/all_gather | solution.py:443
  432.3 217.6 %pair_step.4 = (f32[4864,3072]{1,0:T(8,128)}, f32[49152,128]{1,0:T(8,128)}, f32[24,128]{1,0:T(8,128)}) custom-call(s32[73856]{0:T(1024)S(1)} %concatenate.32.pay_ref, s32[65]{0:T(128)} %convert_reduce_fusion.1.start_ref, f32[49152,128]{1,0:T(8,128)} %to_rows.2.table_ref.acc_ref, f32[49152,128]{1,0:T(8,128)} %get-tuple-element.82.acc_ref, ...), custom_call_target="tpu_custom_call" | custom-call | flops 38400000000 | bytes 384000000 | tf_op jit(solution)/shard_map/pair_step/pallas_call | solution.py:318
  650.6 1.1 pad_add_fusion.7.base_ref
  651.7 1.1 pad_add_fusion.6.base_ref
  655.3 56.2 %psum.14 = f32[]{:T(128)} all-reduce(f32[]{:T(128)S(6)} %add.221), channel_id=1, replica_groups=mesh['ep'=16] {'ep'}, use_global_device_ids=true, to_apply=%region_17.18 | all-reduce | flops 1 | bytes 8 | tf_op jit(solution)/shard_map/psum | solution.py:453
  711.5 22.9 %from_rows.3 = f32[300,16384]{1,0:T(8,128)} custom-call(f32[49152,128]{1,0:T(8,128)} %get-tuple-element.85.x_ref), custom_call_target="tpu_custom_call" | custom-call | flops 2200000000 | bytes 22000000 | tf_op jit(solution)/shard_map/from_rows/pallas_call | solution.py:67
  734.4 36.6 %u_update.2.table_ref = f32[49152,128]{1,0:T(8,128)} custom-call(s32[66304]{0:T(1024)S(1)} %concatenate.25.pay_ref, s32[2]{0:T(128)} %pad_add_fusion.7.base_ref, f32[300,16384]{1,0:T(8,128)} %bitcast.66, f32[304,1920]{1,0:T(8,128)} %reduce-scatter.4.cloned.1.call-done.rest_0_), custom_call_target="tpu_custom_call" | custom-call | flops 4499999744 | bytes 45000000 | tf_op jit(solution)/shard_map/u_update/pallas_call | solution.py:154
  771.1 185.9 %reduce-scatter.6.cloned.1.call-done.g_ref = f32[304,3072]{1,0:T(8,128)} async-done(((f32[4864,3072]{1,0:T(8,128)}), f32[304,3072]{1,0:T(8,128)}) %reduce-scatter.6.cloned.1.call-update) | async-done | bytes 3735568 | tf_op jit(solution)/shard_map/reduce_scatter | solution.py:446
  956.9 36.8 %u_finish.1 = f32[300,16384]{1,0:T(8,128)} custom-call(s32[66304]{0:T(1024)S(1)} %concatenate.25.pay_ref, s32[2]{0:T(128)} %pad_add_fusion.6.base_ref, f32[49152,128]{1,0:T(8,128)} %u_update.2.table_ref, f32[304,3072]{1,0:T(8,128)} %reduce-scatter.6.cloned.1.call-done.g_ref), custom_call_target="tpu_custom_call" | custom-call | flops 3000000000 | bytes 30000000 | tf_op jit(solution)/shard_map/u_finish/pallas_call | solution.py:189
  (92 shorter events, 18.0 us)
Async XLA Ops:
  7.2 59.1 %copy-start.1 = (s32[4096]{0:T(1024)S(1)}, s32[4096]{0:T(1024)}, u32[]{:S(2)}) copy-start(s32[4096]{0:T(1024)} %param.9) | copy-start | bytes 49156
  7.2 60.1 %copy-start.2 = (s32[4096]{0:T(1024)S(1)}, s32[4096]{0:T(1024)}, u32[]{:S(2)}) copy-start(s32[4096]{0:T(1024)} %param.10) | copy-start | bytes 49156
  7.2 60.1 %copy-start = (s32[4096,10]{0,1:T(8,128)S(1)}, s32[4096,10]{0,1:T(8,128)}, u32[]{:S(2)}) copy-start(s32[4096,10]{0,1:T(8,128)} %param.11) | copy-start | bytes 491524
  7.2 211.3 %all-gather.4.cloned.1.call-start = ((), (), s32[]{:S(2)}) async-start(), calls=%async_computation.4 | async-start | bytes 39690240 | tf_op jit(solution)/shard_map/all_gather | solution.py:443
  65.5 366.8 %all-gather.6.cloned.1.call-start = ((), (), s32[]{:S(2)}) async-start(), calls=%async_computation.6 | async-start | bytes 63504384 | tf_op jit(solution)/shard_map/all_gather | solution.py:443
  116.5 49.0 %all-to-all-start = ((s32[16,1,4608]{2,1,0:T(1,128)}), s32[16,1,4608]{2,1,0:T(1,128)S(1)}, u32[]{:S(2)}, u32[]{:S(2)}) async-start(s32[16,1,4608]{2,1,0:T(1,128)} %bitcast.12), calls=%async_computation.1 | async-start | bytes 589824 | tf_op jit(solution)/shard_map/all_to_all | solution.py:400
  118.8 615.6 %reduce-scatter.4.cloned.1.call-start = ((), (), s32[]{:S(2)}) async-start(), calls=%async_computation.5 | async-start | bytes 39690240 | tf_op jit(solution)/shard_map/reduce_scatter | solution.py:446
  413.2 543.7 %reduce-scatter.6.cloned.1.call-start = ((), (), s32[]{:S(2)}) async-start(), calls=%async_computation.7 | async-start | bytes 63504384 | tf_op jit(solution)/shard_map/reduce_scatter | solution.py:446
  649.9 2.9 copy-start.3
  649.9 3.5 copy-start.4
Sparse Core Ops, SparseCore 0:
  65.6 146.7 all-gather.3
  215.3 217.0 all-gather.5
  437.4 200.6 reduce-scatter.3
  650.1 306.8 reduce-scatter.5
